TPU v7x, 128 devices: a whole 4x4x4 slice. The times are simulated.
128 devices in a mesh: seq: 16 (over y, x_hi, core), head: 8 (over z, x_lo).
Axes of the slice: x: 4 (x_hi: 2, x_lo: 2; x = x_hi * 2 + x_lo), y: 4, z: 4, core: 2. Of those that a mesh axis runs over, the one named last changes fastest.
Arguments:
- d_bytes: bfloat16 [4096, 8192], P('seq', 'head'), may hold values from -6 to 6
- owner_groups: int32 [16, 16], replicated, may hold values from 0 to 255, as said below
- block_order: int32 [16], replicated, may hold values from 0 to 15, each once
- y_in: bfloat16 [4096, 4096], P('seq'), may hold values from -0.29882812 to 0.29882812
- w_proj: bfloat16 [4096, 8192], P('seq', 'head'), may hold values from -0.0625 to 0.0625
- w_out: bfloat16 [2048, 4096], P('head', 'seq'), may hold values from -0.125 to 0.125
- queries: bfloat16 [4096, 2048], P('seq', 'head'), may hold values from -24 to 24
- keys: bfloat16 [4096, 2048], P('seq', 'head'), may hold values from -24 to 24
- values: bfloat16 [4096, 2048], P('seq', 'head'), may hold values from -6 to 6
- attn_out: bfloat16 [4096, 2048], P('seq', 'head'), may hold values from -0.59765625 to 0.59765625
Outputs:
- layer_grad: bfloat16 [4096, 4096], P('seq', 'head')
- grad_proj: bfloat16 [4096, 8192], P('seq', 'head')
- grad_out: bfloat16 [2048, 4096], P('head', 'seq')
- grad_queries: bfloat16 [4096, 2048], P('seq', 'head')
- grad_keys: bfloat16 [4096, 2048], P('seq', 'head')
- grad_values: bfloat16 [4096, 2048], P('seq', 'head')
Inputs may be any that keep to these rules, and one draw needn't show every extreme that they name: `owner_groups`: row o lists the patch groups held by owner o; it holds exactly one group of every seq shard (group g covers patches g * 16 to g * 16 + 15, shard g // 16), and every group appears once. `block_order`: A permutation.
All inputs are finite; a program needn't handle non-finite values.
Results may differ from a plain program's by a relative error of at most 0.03.
Values may be sent and summed in bfloat16 or wider, within the bound.
No kernel may reach another device: no remote copies, remote signals or barrier semaphores. Data moves between devices by JAX's collectives and lax.ppermute only.
A program may use at most 128 MiB of HBM per device.

v0:
```python
import math
import jax
import jax.numpy as jnp
from jax import lax
from jax.sharding import PartitionSpec as P

HEAD_DIM = 128


def in_blocks(shard, dim, peers):
    before, after = (shard.shape[:dim], shard.shape[dim + 1 :])
    return jnp.moveaxis(shard.reshape(*before, peers, -1, *after), dim, 0)


def summed_on_arrival(shard, axis, dim):
    pieces = in_blocks(shard, dim, lax.axis_size(axis))
    arrived = lax.all_to_all(pieces, axis, split_axis=0, concat_axis=0, tiled=True)
    return arrived.astype(jnp.float32).sum(axis=0)


def in_order(pieces, dim):
    shape = list(pieces.shape[1:])
    shape[dim] *= pieces.shape[0]
    return jnp.moveaxis(pieces, 0, dim).reshape(shape)


def from_everyone(shard, axis):
    peers = lax.axis_size(axis)
    return lax.all_to_all(
        jnp.broadcast_to(shard[None], (peers, *shard.shape)), axis, 0, 0, tiled=True
    )


def gathered_copies(shard, axis, dim):
    return in_order(from_everyone(shard, axis), dim)


def in_one_piece(arrays, axis, dim, along):
    both = jnp.concatenate(arrays, axis=along)
    filled, at, gathered = (lax.all_gather(both, axis, axis=dim, tiled=True), 0, [])
    for a in arrays:
        gathered.append(lax.slice_in_dim(filled, at, at + a.shape[along], axis=along))
        at += a.shape[along]
    return tuple(gathered)


def sent_together(arrays, axis, dim, along):
    ends, at = ([], 0)
    for a in arrays[:-1]:
        at += a.shape[along]
        ends.append(at)
    both = jnp.concatenate(arrays, axis=along)
    return tuple(
        jnp.split(lax.psum_scatter(both, axis, scatter_dimension=dim, tiled=True), ends, axis=along)
    )


def body(d_bytes, owner_groups, block_order, y_in, w_proj, w_out, queries, keys, values, attn_out):
    flt = jnp.float32
    half = jnp.bfloat16
    owners = lax.axis_size("seq")
    seq_index = lax.axis_index("seq")
    patch_dev = y_in.shape[0]
    group_rows = patch_dev // owners
    columns = d_bytes.shape[1]
    owner_ids = jnp.arange(owners, dtype=jnp.int32)
    mine = jnp.sum(jnp.where(owner_ids[:, None] == seq_index, owner_groups, 0), axis=0)
    sending = jnp.argsort(mine // owners)
    outgoing = jnp.take(d_bytes.reshape(owners, group_rows, columns), sending, axis=0)
    incoming = lax.all_to_all(outgoing, "seq", split_axis=0, concat_axis=0, tiled=True)
    landing = jnp.sum(
        jnp.where(owner_groups // owners == seq_index, owner_groups % owners, 0), axis=1
    )
    arrival = jnp.argsort(landing)
    natural = jnp.take(incoming, arrival, axis=0).reshape(patch_dev, columns)
    grad_proj = (
        lax.psum_scatter(
            lax.dot_general(
                y_in, natural, (((0,), (0,)), ((), ())), preferred_element_type=flt
            ).astype(jnp.bfloat16),
            "seq",
            scatter_dimension=0,
            tiled=True,
        )
        .astype(jnp.float32)
        .astype(half)
    )
    head_part = lax.dot_general(
        natural,
        lax.all_gather(w_proj, "seq", axis=0, tiled=True),
        (((1,), (1,)), ((), ())),
        preferred_element_type=flt,
    )
    layer_grad = summed_on_arrival(head_part.astype(jnp.bfloat16), "head", 1).astype(half)
    full_grad = gathered_copies(layer_grad, "head", 1)
    width_dev = queries.shape[1]
    attn_grad = lax.dot_general(
        full_grad,
        lax.all_gather(w_out, "seq", axis=1, tiled=True),
        (((1,), (1,)), ((), ())),
        preferred_element_type=flt,
    ).astype(half)
    out_term = lax.dot_general(
        attn_out, full_grad, (((0,), (0,)), ((), ())), preferred_element_type=flt
    )
    grad_out = summed_on_arrival(out_term.astype(jnp.bfloat16), "seq", 1).astype(half)
    heads_dev = width_dev // HEAD_DIM
    scale = 1.0 / math.sqrt(HEAD_DIM)
    query_heads = queries.reshape(patch_dev, heads_dev, HEAD_DIM)
    grad_heads = attn_grad.reshape(patch_dev, heads_dev, HEAD_DIM)
    delta = jnp.sum(
        grad_heads.astype(flt) * attn_out.reshape(patch_dev, heads_dev, HEAD_DIM).astype(flt),
        axis=2,
    ).T
    local_rows = jnp.arange(patch_dev, dtype=jnp.int32)
    my_block = jnp.sum(jnp.where(owner_ids == seq_index, block_order, 0))
    query_pos = my_block * patch_dev + local_rows
    keys_all, values_all = in_one_piece((keys, values), "seq", 0, 1)
    all_rows = keys_all.shape[0]
    block_rows = math.gcd(512, all_rows)
    block_count = all_rows // block_rows
    row_ids = jnp.arange(all_rows, dtype=jnp.int32)
    row_owner = row_ids // patch_dev
    key_pos = (
        jnp.sum(
            jnp.where(row_owner[:, None] == owner_ids[None, :], block_order[None, :], 0), axis=1
        )
        * patch_dev
        + row_ids % patch_dev
    )
    key_blocks = keys_all.reshape(block_count, block_rows, heads_dev, HEAD_DIM)
    value_blocks = values_all.reshape(block_count, block_rows, heads_dev, HEAD_DIM)
    pos_blocks = key_pos.reshape(block_count, block_rows)

    def scores_of(key_block, pos_block):
        scores = (
            jnp.einsum("qhd,khd->hqk", query_heads, key_block, preferred_element_type=flt) * scale
        )
        allowed = pos_block[None, :] <= query_pos[:, None]
        return (scores, allowed)

    def statistics(running, pieces):
        highest, totals = running
        key_block, pos_block = pieces
        scores, allowed = scores_of(key_block, pos_block)
        scores = jnp.where(allowed[None], scores, -1e30)
        new_high = jnp.maximum(highest, jnp.max(scores, axis=2))
        weights = jnp.where(allowed[None], jnp.exp(scores - new_high[:, :, None]), 0.0)
        totals = totals * jnp.exp(highest - new_high) + jnp.sum(weights, axis=2)
        return ((new_high, totals), None)

    start_stats = (
        jnp.full((heads_dev, patch_dev), -1e30, flt),
        jnp.zeros((heads_dev, patch_dev), flt),
    )
    (highest, totals), _ = lax.scan(statistics, start_stats, (key_blocks, pos_blocks))
    log_total = highest + jnp.log(totals)

    def backward(grad_query, pieces):
        key_block, value_block, pos_block = pieces
        scores, allowed = scores_of(key_block, pos_block)
        weights = jnp.where(allowed[None], jnp.exp(scores - log_total[:, :, None]), 0.0)
        grad_weights = jnp.einsum(
            "qhd,khd->hqk", grad_heads, value_block, preferred_element_type=flt
        )
        grad_scores = (weights * (grad_weights - delta[:, :, None]) * scale).astype(half)
        weights_low = weights.astype(half)
        grad_query = grad_query + jnp.einsum(
            "hqk,khd->qhd", grad_scores, key_block, preferred_element_type=flt
        )
        key_term = jnp.einsum("hqk,qhd->khd", grad_scores, query_heads, preferred_element_type=flt)
        value_term = jnp.einsum("hqk,qhd->khd", weights_low, grad_heads, preferred_element_type=flt)
        return (grad_query, (key_term, value_term))

    start_grad = jnp.zeros((patch_dev, heads_dev, HEAD_DIM), flt)
    grad_query, (key_terms, value_terms) = lax.scan(
        backward, start_grad, (key_blocks, value_blocks, pos_blocks)
    )
    key_terms = key_terms.reshape(all_rows, width_dev)
    value_terms = value_terms.reshape(all_rows, width_dev)
    grad_keys, grad_values = tuple(
        (
            part.astype(jnp.float32)
            for part in sent_together(
                (key_terms.astype(jnp.bfloat16), value_terms.astype(jnp.bfloat16)), "seq", 0, 1
            )
        )
    )
    grad_queries = grad_query.reshape(patch_dev, width_dev).astype(half)
    return (
        layer_grad,
        grad_proj,
        grad_out,
        grad_queries,
        grad_keys.astype(half),
        grad_values.astype(half),
    )


def solution(mesh):
    placed = (
        P("seq", "head"),
        P(),
        P(),
        P("seq", None),
        P("seq", "head"),
        P("head", "seq"),
        P("seq", "head"),
        P("seq", "head"),
        P("seq", "head"),
        P("seq", "head"),
    )
    return jax.shard_map(
        body,
        mesh=mesh,
        in_specs=placed,
        out_specs=(
            P("seq", "head"),
            P("seq", "head"),
            P("head", "seq"),
            P("seq", "head"),
            P("seq", "head"),
            P("seq", "head"),
        ),
        check_vma=False,
    )
```

profile of v0, /device:TPU:0, one launch (start us, length us, event | category | flops | bytes accessed | tf_op | source)
XLA Modules:
  0.0 408.7 jit_solution(1989037170501856111)
XLA Ops:
  15.2 7.1 %all-to-all-start = ((bf16[16,16,1024]{2,1,0:T(8,128)(2,1)}), bf16[16,16,1024]{2,1,0:T(8,128)(2,1)S(1)}, u32[]{:S(2)}, u32[]{:S(2)}) async-start(bf16[16,16,1024]{2,1,0:T(8,128)(2,1)} %broadcast_select_fusion.2), calls=%async_computation | async-start | bytes 1048576 | tf_op jit(solution)/shard_map/all_to_all | solution.py:70
  23.8 16.4 %all-to-all-done = bf16[16,16,1024]{2,1,0:T(8,128)(2,1)S(1)} async-done(((bf16[16,16,1024]{2,1,0:T(8,128)(2,1)}), bf16[16,16,1024]{2,1,0:T(8,128)(2,1)S(1)}, u32[]{:S(2)}, u32[]{:S(2)}) %all-to-all-start) | async-done | bytes 524320 | tf_op jit(solution)/shard_map/all_to_all | solution.py:70
  40.9 49.9 %all-gather.4.cloned.1.call-done = bf16[4096,1024]{1,0:T(8,128)(2,1)} async-done(((bf16[256,1024]{1,0:T(8,128)(2,1)}), bf16[4096,1024]{1,0:T(8,128)(2,1)}) %all-gather.4.cloned.1.call-update) | async-done | bytes 8388624 | tf_op jit(solution)/shard_map/all_gather | solution.py:90
  90.8 5.8 %convolution_convert_fusion = bf16[256,4096]{1,0:T(8,128)(2,1)S(1)} fusion(bf16[256,1024]{1,0:T(8,128)(2,1)S(1)} %bitcast.139, bf16[4096,1024]{1,0:T(8,128)(2,1)} %all-gather.4.cloned.1.call-done), kind=kOutput, calls=%fused_computation.47 | convolution fusion | flops 2148532224 | bytes 11010048 | tf_op jit(solution)/shard_map/dot_general | solution.py:88
  98.1 4.6 %all-to-all-start.1 = ((bf16[8,256,512]{2,1,0:T(8,128)(2,1)}), bf16[8,256,512]{2,1,0:T(8,128)(2,1)}, u32[]{:S(2)}, u32[]{:S(2)}) async-start(bf16[8,256,512]{2,1,0:T(8,128)(2,1)} %bitcast.135), calls=%async_computation.1 | async-start | bytes 4194304 | tf_op jit(solution)/shard_map/all_to_all | solution.py:17
  105.7 5.6 %convert_bitcast_fusion = bf16[4096,1024]{0,1:T(8,128)(2,1)} fusion(bf16[256,1024]{1,0:T(8,128)(2,1)S(1)} %bitcast.140, bf16[256,4096]{1,0:T(8,128)(2,1)S(1)} %copy-done), kind=kOutput, calls=%fused_computation.46 | convolution fusion | flops 2151677952 | bytes 11010048 | tf_op jit(solution)/shard_map/dot_general | solution.py:78
  111.3 38.1 %all-gather.6.cloned.1.call-done = bf16[4096,512]{1,0:T(8,128)(2,1)} async-done(((bf16[256,512]{1,0:T(8,128)(2,1)}), bf16[4096,512]{1,0:T(8,128)(2,1)}) %all-gather.6.cloned.1.call-update) | async-done | bytes 4194320 | tf_op jit(solution)/shard_map/all_gather | solution.py:40
  149.4 4.5 %fusion.40 = (bf16[4096,256]{1,0:T(8,128)(2,1)}, bf16[4096,256]{1,0:T(8,128)(2,1)}) fusion(bf16[4096,512]{1,0:T(8,128)(2,1)} %all-gather.6.cloned.1.call-done), kind=kLoop, calls=%fused_computation.99 | loop fusion | bytes 8388608 | tf_op jit(solution)/shard_map/slice | solution.py:42
  154.0 2.5 reshape.169
  158.3 2.0 reduce_sum.80
  161.9 4.8 %all-to-all-start.2 = ((bf16[8,256,512]{1,2,0:T(8,128)(2,1)}), bf16[8,256,512]{1,2,0:T(8,128)(2,1)S(1)}, u32[]{:S(2)}, u32[]{:S(2)}) async-start(bf16[8,256,512]{1,2,0:T(8,128)(2,1)} %broadcast_in_dim.101), calls=%async_computation.3 | async-start | bytes 4194304 | tf_op jit(solution)/shard_map/all_to_all | solution.py:29
  167.0 19.6 %while.28 = (s32[]{:T(128)}, f32[2,256]{1,0:T(2,128)S(1)}, f32[2,256]{1,0:T(2,128)S(1)}, s32[8,512]{1,0:T(8,128)}, bf16[8,512,2,128]{3,1,2,0:T(8,128)(2,1)}, /*i...) while((s32[]{:T(128)}, f32[2,256]{1,0:T(2,128)S(1)}, ...), condition=%wide.region_12.14_spmd.clone, body=%wide.region_9.13_spmd.clone.sunk | while | flops 68815616 | bytes 2918524 | solution.py:156
  186.6 4.1 reshape.170
  190.7 12.7 %all-gather.8.cloned.1.call-done = bf16[256,4096]{1,0:T(8,128)(2,1)} async-done(((bf16[256,256]{1,0:T(8,128)(2,1)}), bf16[256,4096]{1,0:T(8,128)(2,1)}) %all-gather.8.cloned.1.call-update) | async-done | bytes 2097168 | tf_op jit(solution)/shard_map/all_gather | solution.py:99
  203.4 3.1 multiply_reduce_fusion
  206.6 55.9 %while.29 = (s32[]{:T(128)}, f32[256,2,128]{0,2,1:T(8,128)S(1)}, bf16[8,512,2,128]{3,1,2,0:T(8,128)(2,1)}, bf16[8,512,2,128]{3,1,2,0:T(8,128)(2,1)}, bf16[8,512,...) while((s32[]{:T(128)}, f32[256,2,128]{0,2,1:T(8,128)S(1)}, ...), condition=%wide.region_15.17_spmd.clone, body=%wide.region_14.16_spmd.clone.sunk | while | flops 337903872 | bytes 8401075 | solution.py:176
  262.5 3.9 copy.76
  266.4 2.2 copy.75
  269.4 2.3 pad_maximum_fusion
  273.3 2.0 convolution_convert_fusion.1
  275.4 4.5 %all-to-all-start.3 = ((bf16[16,256,256]{1,2,0:T(8,128)(2,1)}), bf16[16,256,256]{1,2,0:T(8,128)(2,1)}, u32[]{:S(2)}, u32[]{:S(2)}) async-start(bf16[16,256,256]{1,2,0:T(8,128)(2,1)} %bitcast.134), calls=%async_computation.4 | async-start | bytes 4194304 | tf_op jit(solution)/shard_map/all_to_all | solution.py:17
  279.8 37.9 %reduce-scatter.3.cloned.1.call-done = bf16[256,1024]{0,1:T(8,128)(2,1)} async-done(((bf16[4096,1024]{0,1:T(8,128)(2,1)}), bf16[256,1024]{0,1:T(8,128)(2,1)}) %reduce-scatter.3.cloned.1.call-update) | async-done | bytes 524304 | tf_op jit(solution)/shard_map/reduce_scatter | solution.py:77
  317.7 2.2 copy.77
  323.3 77.2 %reduce-scatter.5.cloned.1.call-done = bf16[256,512]{1,0:T(8,128)(2,1)} async-done(((bf16[4096,512]{1,0:T(8,128)(2,1)}), bf16[256,512]{1,0:T(8,128)(2,1)}) %reduce-scatter.5.cloned.1.call-update) | async-done | bytes 262160 | tf_op jit(solution)/shard_map/reduce_scatter | solution.py:54
  (219 shorter events, 99.9 us)
Async XLA Ops:
  7.2 98.5 %copy-start = (bf16[256,4096]{1,0:T(8,128)(2,1)S(1)}, bf16[256,4096]{1,0:T(8,128)(2,1)}, u32[]{:S(2)}) copy-start(bf16[256,4096]{1,0:T(8,128)(2,1)} %param.19) | copy-start | bytes 6291460
  7.2 83.6 %all-gather.4.cloned.1.call-start = ((), (), s32[]{:S(2)}) async-start(), calls=%async_computation.6 | async-start | bytes 8912896 | tf_op jit(solution)/shard_map/all_gather | solution.py:90
  7.9 15.7 %copy-start.12 = (s32[16]{0:T(128)S(1)}, s32[16]{0:T(128)}, u32[]{:S(2)}) copy-start(s32[16]{0:T(128)} %param.18) | copy-start | bytes 196
  7.9 141.5 %all-gather.6.cloned.1.call-start = ((), (), s32[]{:S(2)}) async-start(), calls=%async_computation.8 | async-start | bytes 4456448 | tf_op jit(solution)/shard_map/all_gather | solution.py:40
  9.7 193.7 %all-gather.8.cloned.1.call-start = ((), (), s32[]{:S(2)}) async-start(), calls=%async_computation.9 | async-start | bytes 2228224 | tf_op jit(solution)/shard_map/all_gather | solution.py:99
  15.2 25.0 %all-to-all-start = ((bf16[16,16,1024]{2,1,0:T(8,128)(2,1)}), bf16[16,16,1024]{2,1,0:T(8,128)(2,1)S(1)}, u32[]{:S(2)}, u32[]{:S(2)}) async-start(bf16[16,16,1024]{2,1,0:T(8,128)(2,1)} %broadcast_select_fusion.2), calls=%async_computation | async-start | bytes 1048576 | tf_op jit(solution)/shard_map/all_to_all | solution.py:70
  40.9 55.7 %copy-start.6 = (bf16[16,16,1024]{2,1,0:T(8,128)(2,1)}, bf16[16,16,1024]{2,1,0:T(8,128)(2,1)S(1)}, u32[]{:S(2)}) copy-start(bf16[16,16,1024]{2,1,0:T(8,128)(2,1)S(1)} %broadcast_select_fusion.1) | copy-start | bytes 1572868
  98.1 5.3 %copy-start.11 = (bf16[256,256]{1,0:T(8,128)(2,1)S(1)}, bf16[256,256]{1,0:T(8,128)(2,1)}, u32[]{:S(2)}) copy-start(bf16[256,256]{1,0:T(8,128)(2,1)} %param.22) | copy-start | bytes 393220
  98.1 5.5 %copy-start.10 = (bf16[256,256]{1,0:T(8,128)(2,1)S(1)}, bf16[256,256]{1,0:T(8,128)(2,1)}, u32[]{:S(2)}) copy-start(bf16[256,256]{1,0:T(8,128)(2,1)} %param.25) | copy-start | bytes 393220
  98.1 7.6 %copy-start.7 = (bf16[16,16,1024]{2,1,0:T(8,128)(2,1)S(1)}, bf16[16,16,1024]{2,1,0:T(8,128)(2,1)}, u32[]{:S(2)}) copy-start(bf16[16,16,1024]{2,1,0:T(8,128)(2,1)} %copy-done.6) | copy-start | bytes 1572868
  98.1 60.2 %all-to-all-start.1 = ((bf16[8,256,512]{2,1,0:T(8,128)(2,1)}), bf16[8,256,512]{2,1,0:T(8,128)(2,1)}, u32[]{:S(2)}, u32[]{:S(2)}) async-start(bf16[8,256,512]{2,1,0:T(8,128)(2,1)} %bitcast.135), calls=%async_computation.1 | async-start | bytes 4194304 | tf_op jit(solution)/shard_map/all_to_all | solution.py:17
  102.7 215.0 %reduce-scatter.3.cloned.1.call-start = ((), (), s32[]{:S(2)}) async-start(), calls=%async_computation.7 | async-start | bytes 8912896 | tf_op jit(solution)/shard_map/reduce_scatter | solution.py:77
  160.3 1.7 copy-start.8
  161.9 41.4 %all-to-all-start.2 = ((bf16[8,256,512]{1,2,0:T(8,128)(2,1)}), bf16[8,256,512]{1,2,0:T(8,128)(2,1)S(1)}, u32[]{:S(2)}, u32[]{:S(2)}) async-start(bf16[8,256,512]{1,2,0:T(8,128)(2,1)} %broadcast_in_dim.101), calls=%async_computation.3 | async-start | bytes 4194304 | tf_op jit(solution)/shard_map/all_to_all | solution.py:29
  166.8 233.7 %reduce-scatter.5.cloned.1.call-start = ((), (), s32[]{:S(2)}) async-start(), calls=%async_computation.10 | async-start | bytes 4456448 | tf_op jit(solution)/shard_map/reduce_scatter | solution.py:54
  186.6 16.7 %copy-start.9 = (f32[256,256]{0,1:T(8,128)S(1)}, f32[256,256]{0,1:T(8,128)}, u32[]{:S(2)}) copy-start(f32[256,256]{0,1:T(8,128)} %copy.86) | copy-start | bytes 786436
  203.4 3.1 copy-start.2
  203.4 3.2 copy-start.4
  262.5 3.9 copy-start.5
  271.7 1.6 copy-start.3
  275.4 45.3 %all-to-all-start.3 = ((bf16[16,256,256]{1,2,0:T(8,128)(2,1)}), bf16[16,256,256]{1,2,0:T(8,128)(2,1)}, u32[]{:S(2)}, u32[]{:S(2)}) async-start(bf16[16,256,256]{1,2,0:T(8,128)(2,1)} %bitcast.134), calls=%async_computation.4 | async-start | bytes 4194304 | tf_op jit(solution)/shard_map/all_to_all | solution.py:17
  317.7 84.5 %copy-start.1 = (bf16[256,4096]{1,0:T(8,128)(2,1)S(1)}, bf16[256,4096]{1,0:T(8,128)(2,1)}, u32[]{:S(2)}) copy-start(bf16[256,4096]{1,0:T(8,128)(2,1)} %param.19) | copy-start | bytes 6291460
Sparse Core Ops, SparseCore 0:
  10.5 80.3 all-gather.3
  93.9 55.5 all-gather.5
  151.8 51.5 all-gather.7
  207.5 110.1 reduce-scatter.2
  321.5 78.9 reduce-scatter.4
where the time goes:
time: 411 us; the launch traced here: 409 us
  waiting for transfers between devices  234 us (57%)
  matrix products  66 us (16%)
  local copies, waits for them, and re-layouts  54.2 us (13%)
  starting transfers between devices  21.3 us (5%)
  other arithmetic  18.1 us (4%)
  between operations  14.7 us (4%)
    reduce_scatter x1, waiting for transfers between devices, sent_together(): lax.psum_scatter(both, axis, scatter_dimension=dim, tiled=True)  77.2 us
    all_gather x1, waiting for transfers between devices, body(): lax.all_gather(w_proj, 'seq', axis=0, tiled=True)  49.9 us
    all_gather x1, waiting for transfers between devices, in_one_piece(): lax.all_gather(both, axis, axis=dim, tiled=True)  38.1 us
    reduce_scatter x1, waiting for transfers between devices, body(): lax.psum_scatter(lax.dot_general(y_in, natural, (((0,), (0,)), ((), ())),...  37.9 us
    dynamic_slice x24, local copies, waits for them, and re-layouts, body(): lax.scan(statistics, start_stats, (key_blocks, pos_blocks))  20.8 us
    dot_general x16, matrix products, scores_of(): jnp.einsum('qhd,khd->hqk', query_heads, key_block, preferred_element_type...  20.8 us
    all_to_all x1, waiting for transfers between devices, body(): lax.all_to_all(outgoing, 'seq', split_axis=0, concat_axis=0, tiled=True)  16.4 us
    all_gather x1, waiting for transfers between devices, body(): lax.all_gather(w_out, 'seq', axis=1, tiled=True)  12.7 us
  transfers between devices with their start and end apart: 9, of which 6 were waited for; matrix products, arithmetic and copies ran while one was open for 33% of the time, Pallas kernels for 0%

commit v1 on v0

--- a/solution.py
+++ b/solution.py
@@ -87,7 +87,9 @@
     )
     head_part = lax.dot_general(
         natural,
-        lax.all_gather(w_proj, "seq", axis=0, tiled=True),
+        jnp.concatenate(
+            lax.all_to_all(jnp.stack([w_proj] * lax.axis_size("seq")), "seq", 0, 0), axis=0
+        ),
         (((1,), (1,)), ((), ())),
         preferred_element_type=flt,
     )

time: 411 us -> 388 us (0.944)
  waiting for transfers between devices: 234 us -> 197 us
  blocking collectives: 0 us -> 22.1 us
  local copies, waits for them, and re-layouts: 54.2 us -> 45.4 us
    all_to_all x1, waiting for transfers between devices: 16.4 us -> 106 us  [body(): lax.all_to_all(jnp.stack([w_proj] * lax.axis_size('seq')), 'seq', 0, 0)]
    all_gather x1 -> x0, waiting for transfers between devices: 49.9 us -> none  [body(): lax.all_gather(w_proj, 'seq', axis=0, tiled=True)]
    reduce_scatter x1, waiting for transfers between devices: 77.2 us -> 38.5 us  [sent_together(): lax.psum_scatter(both, axis, scatter_dimension=dim, tiled=True)]
    all_gather x1, waiting for transfers between devices: 38.1 us -> 0.02 us  [in_one_piece(): lax.all_gather(both, axis, axis=dim, tiled=True)]
    reduce_scatter x1, waiting for transfers between devices: 37.9 us -> 0.01 us  [body(): lax.psum_scatter(lax.dot_general(y_in, natural, (((0,), (0,)), ((), ())),...]
    all_to_all x2, waiting for transfers between devices: 0.01 us -> 37.2 us  [summed_on_arrival(): lax.all_to_all(pieces, axis, split_axis=0, concat_axis=0, tiled=True)]
    all_to_all x0 -> x1, blocking collectives: none -> 22.1 us  [body(): lax.all_to_all(outgoing, 'seq', split_axis=0, concat_axis=0, tiled=True)]
    all_to_all x1, waiting for transfers between devices: 0.01 us -> 14.1 us  [from_everyone(): lax.all_to_all(jnp.broadcast_to(shard[None], (peers, *shard.shape)), axis...]
  transfers between devices with their start and end apart: 9 -> 8, of which waited for: 6 -> 5; matrix products, arithmetic and copies ran while one was open for 33% -> 33% of each run, Pallas kernels for 0% -> 0%
where the time goes in v1:
time: 388 us; the launch traced here: 386 us
  waiting for transfers between devices  197 us (51%)
  matrix products  67.4 us (17%)
  local copies, waits for them, and re-layouts  45.4 us (12%)
  blocking collectives  22.1 us (6%)
  starting transfers between devices  21.5 us (6%)
  other arithmetic  17.7 us (5%)
  between operations  14.7 us (4%)
    all_to_all x1, waiting for transfers between devices, body(): lax.all_to_all(jnp.stack([w_proj] * lax.axis_size('seq')), 'seq', 0, 0)  106 us
    reduce_scatter x1, waiting for transfers between devices, sent_together(): lax.psum_scatter(both, axis, scatter_dimension=dim, tiled=True)  38.5 us
    all_to_all x2, waiting for transfers between devices, summed_on_arrival(): lax.all_to_all(pieces, axis, split_axis=0, concat_axis=0, tiled=True)  37.2 us
    all_to_all x1, blocking collectives, body(): lax.all_to_all(outgoing, 'seq', split_axis=0, concat_axis=0, tiled=True)  22.1 us
    dot_general x16, matrix products, scores_of(): jnp.einsum('qhd,khd->hqk', query_heads, key_block, preferred_element_type...  20.8 us
    all_to_all x1, waiting for transfers between devices, from_everyone(): lax.all_to_all(jnp.broadcast_to(shard[None], (peers, *shard.shape)), axis...  14.1 us
    all_to_all x2, starting transfers between devices, summed_on_arrival(): lax.all_to_all(pieces, axis, split_axis=0, concat_axis=0, tiled=True)  12 us
    dot_general x8, matrix products, backward(): jnp.einsum('hqk,khd->qhd', grad_scores, key_block, preferred_element_type...  10.1 us
  transfers between devices with their start and end apart: 8, of which 5 were waited for; matrix products, arithmetic and copies ran while one was open for 33% of the time, Pallas kernels for 0%

profile of v1, /device:TPU:0, one launch (start us, length us, event | category | flops | bytes accessed | tf_op | source)
XLA Modules:
  0.0 386.2 jit_solution(10437219438366620825)
XLA Ops:
  13.1 22.1 %all_to_all.25 = bf16[16,16,1024]{2,1,0:T(8,128)(2,1)S(1)} all-to-all(bf16[16,16,1024]{2,1,0:T(8,128)(2,1)S(1)} %broadcast_select_fusion.2), channel_id=1, replica_groups=mesh['seq'=16,'head'=8] {'seq'}, dimensions={0} | all-to-all | bytes 1048576 | tf_op jit(solution)/shard_map/all_to_all | solution.py:70
  35.2 4.3 %stack.2 = bf16[16,256,1024]{2,1,0:T(8,128)(2,1)} broadcast(bf16[256,1024]{1,0:T(8,128)(2,1)S(1)} %copy-done.7), dimensions={1,2} | broadcast | bytes 8912896 | tf_op jit(solution)/shard_map/stack | solution.py:91
  39.5 4.9 %all-to-all-start.1 = ((bf16[16,256,1024]{2,1,0:T(8,128)(2,1)}), bf16[16,256,1024]{2,1,0:T(8,128)(2,1)}, u32[]{:S(2)}, u32[]{:S(2)}) async-start(bf16[16,256,1024]{2,1,0:T(8,128)(2,1)} %stack.2), calls=%async_computation.1 | async-start | bytes 16777216 | tf_op jit(solution)/shard_map/all_to_all | solution.py:91
  47.9 106.0 %all-to-all-done.1 = bf16[16,256,1024]{2,1,0:T(8,128)(2,1)} async-done(((bf16[16,256,1024]{2,1,0:T(8,128)(2,1)}), bf16[16,256,1024]{2,1,0:T(8,128)(2,1)}, u32[]{:S(2)}, u32[]{:S(2)}) %all-to-all-start.1) | async-done | bytes 8388640 | tf_op jit(solution)/shard_map/all_to_all | solution.py:91
  153.8 5.8 %convolution_convert_fusion = bf16[256,4096]{1,0:T(8,128)(2,1)S(1)} fusion(bf16[256,1024]{1,0:T(8,128)(2,1)S(1)} %bitcast.137, bf16[4096,1024]{1,0:T(8,128)(2,1)} %bitcast.2), kind=kOutput, calls=%fused_computation.47 | convolution fusion | flops 2148532224 | bytes 11010048 | tf_op jit(solution)/shard_map/dot_general | solution.py:88
  161.1 5.5 %all-to-all-start.2 = ((bf16[8,256,512]{2,1,0:T(8,128)(2,1)}), bf16[8,256,512]{2,1,0:T(8,128)(2,1)}, u32[]{:S(2)}, u32[]{:S(2)}) async-start(bf16[8,256,512]{2,1,0:T(8,128)(2,1)} %bitcast.133), calls=%async_computation.2 | async-start | bytes 4194304 | tf_op jit(solution)/shard_map/all_to_all | solution.py:17
  169.0 5.6 %convert_bitcast_fusion = bf16[4096,1024]{0,1:T(8,128)(2,1)} fusion(bf16[256,1024]{1,0:T(8,128)(2,1)S(1)} %bitcast.138, bf16[256,4096]{1,0:T(8,128)(2,1)S(1)} %copy-done), kind=kOutput, calls=%fused_computation.46 | convolution fusion | flops 2151677952 | bytes 11010048 | tf_op jit(solution)/shard_map/dot_general | solution.py:78
  174.7 4.8 %fusion.40 = (bf16[4096,256]{1,0:T(8,128)(2,1)}, bf16[4096,256]{1,0:T(8,128)(2,1)}) fusion(bf16[4096,512]{1,0:T(8,128)(2,1)} %all-gather.3.cloned.1.call-done), kind=kLoop, calls=%fused_computation.99 | loop fusion | bytes 8388608 | tf_op jit(solution)/shard_map/slice | solution.py:42
  179.5 2.5 reshape.175
  183.9 10.6 %all-to-all-done.2 = bf16[8,256,512]{2,1,0:T(8,128)(2,1)} async-done(((bf16[8,256,512]{2,1,0:T(8,128)(2,1)}), bf16[8,256,512]{2,1,0:T(8,128)(2,1)}, u32[]{:S(2)}, u32[]{:S(2)}) %all-to-all-start.2) | async-done | bytes 2097184 | tf_op jit(solution)/shard_map/all_to_all | solution.py:17
  194.5 2.2 reduce_sum.80
  198.3 4.4 %all-to-all-start.3 = ((bf16[8,256,512]{1,2,0:T(8,128)(2,1)}), bf16[8,256,512]{1,2,0:T(8,128)(2,1)}, u32[]{:S(2)}, u32[]{:S(2)}) async-start(bf16[8,256,512]{1,2,0:T(8,128)(2,1)} %broadcast_in_dim.101), calls=%async_computation.4 | async-start | bytes 4194304 | tf_op jit(solution)/shard_map/all_to_all | solution.py:29
  202.9 14.0 %while.28 = (s32[]{:T(128)}, f32[2,256]{1,0:T(2,128)S(1)}, f32[2,256]{1,0:T(2,128)S(1)}, s32[8,512]{1,0:T(8,128)S(1)}, bf16[8,512,2,128]{3,1,2,0:T(8,128)(2,1)},...) while((s32[]{:T(128)}, f32[2,256]{1,0:T(2,128)S(1)}, ...), condition=%wide.region_12.14_spmd.clone, body=%wide.region_9.13_spmd.clone.sunk | while | flops 68815616 | bytes 2919024 | solution.py:158
  216.9 4.0 %reshape.176 = bf16[8,512,2,128]{3,2,1,0:T(2,128)(2,1)} reshape(bf16[4096,256]{1,0:T(8,128)(2,1)} %get-tuple-element.322) | data formatting | bytes 4194304 | tf_op jit(solution)/shard_map/reshape | solution.py:134
  221.0 14.1 %all-to-all-done.3 = bf16[8,256,512]{1,2,0:T(8,128)(2,1)} async-done(((bf16[8,256,512]{1,2,0:T(8,128)(2,1)}), bf16[8,256,512]{1,2,0:T(8,128)(2,1)}, u32[]{:S(2)}, u32[]{:S(2)}) %all-to-all-start.3) | async-done | bytes 2097184 | tf_op jit(solution)/shard_map/all_to_all | solution.py:29
  235.1 3.0 multiply_reduce_fusion
  238.2 49.8 %while.29 = (s32[]{:T(128)}, f32[256,2,128]{0,2,1:T(8,128)S(1)}, bf16[8,512,2,128]{3,1,2,0:T(8,128)(2,1)}, bf16[8,512,2,128]{3,1,2,0:T(8,128)(2,1)}, bf16[8,512,...) while((s32[]{:T(128)}, f32[256,2,128]{0,2,1:T(8,128)S(1)}, ...), condition=%wide.region_15.17_spmd.clone, body=%wide.region_14.16_spmd.clone.sunk | while | flops 337903872 | bytes 8403099 | solution.py:178
  288.0 3.9 %copy.75 = bf16[8,512,2,128]{3,2,1,0:T(2,128)(2,1)S(1)} copy(bf16[8,512,2,128]{3,1,2,0:T(8,128)(2,1)} %get-tuple-element.116) | data formatting | bytes 4194304 | tf_op jit(solution)/shard_map/convert_element_type | solution.py:187
  292.0 2.2 copy.76
  294.9 2.3 pad_maximum_fusion
  297.3 3.6 convolution_convert_fusion.1
  300.9 6.5 %all-to-all-start.4 = ((bf16[16,256,256]{1,2,0:T(8,128)(2,1)}), bf16[16,256,256]{1,2,0:T(8,128)(2,1)}, u32[]{:S(2)}, u32[]{:S(2)}) async-start(bf16[16,256,256]{1,2,0:T(8,128)(2,1)} %bitcast.9), calls=%async_computation.5 | async-start | bytes 4194304 | tf_op jit(solution)/shard_map/all_to_all | solution.py:17
  310.3 26.5 %all-to-all-done.4 = bf16[16,256,256]{1,2,0:T(8,128)(2,1)} async-done(((bf16[16,256,256]{1,2,0:T(8,128)(2,1)}), bf16[16,256,256]{1,2,0:T(8,128)(2,1)}, u32[]{:S(2)}, u32[]{:S(2)}) %all-to-all-start.4) | async-done | bytes 2097184 | tf_op jit(solution)/shard_map/all_to_all | solution.py:17
  339.5 38.5 %reduce-scatter.5.cloned.1.call-done = bf16[256,512]{1,0:T(8,128)(2,1)} async-done(((bf16[4096,512]{1,0:T(8,128)(2,1)}), bf16[256,512]{1,0:T(8,128)(2,1)}) %reduce-scatter.5.cloned.1.call-update) | async-done | bytes 262160 | tf_op jit(solution)/shard_map/reduce_scatter | solution.py:54
  (212 shorter events, 87.4 us)
Async XLA Ops:
  7.2 161.9 %copy-start = (bf16[256,4096]{1,0:T(8,128)(2,1)S(1)}, bf16[256,4096]{1,0:T(8,128)(2,1)}, u32[]{:S(2)}) copy-start(bf16[256,4096]{1,0:T(8,128)(2,1)} %param.19) | copy-start | bytes 6291460
  7.2 28.0 %copy-start.7 = (bf16[256,1024]{1,0:T(8,128)(2,1)S(1)}, bf16[256,1024]{1,0:T(8,128)(2,1)}, u32[]{:S(2)}) copy-start(bf16[256,1024]{1,0:T(8,128)(2,1)} %param.20) | copy-start | bytes 1572868
  7.2 167.5 %all-gather.3.cloned.1.call-start = ((), (), s32[]{:S(2)}) async-start(), calls=%async_computation.8 | async-start | bytes 4456448 | tf_op jit(solution)/shard_map/all_gather | solution.py:40
  39.5 6.9 %copy-start.9 = (s32[16]{0:T(128)S(1)}, s32[16]{0:T(128)}, u32[]{:S(2)}) copy-start(s32[16]{0:T(128)} %param.18) | copy-start | bytes 196
  39.5 114.4 %all-to-all-start.1 = ((bf16[16,256,1024]{2,1,0:T(8,128)(2,1)}), bf16[16,256,1024]{2,1,0:T(8,128)(2,1)}, u32[]{:S(2)}, u32[]{:S(2)}) async-start(bf16[16,256,1024]{2,1,0:T(8,128)(2,1)} %stack.2), calls=%async_computation.1 | async-start | bytes 16777216 | tf_op jit(solution)/shard_map/all_to_all | solution.py:91
  44.3 176.6 %all-gather.5.cloned.1.call-start = ((), (), s32[]{:S(2)}) async-start(), calls=%async_computation.9 | async-start | bytes 2228224 | tf_op jit(solution)/shard_map/all_gather | solution.py:101
  47.8 111.8 %copy-start.3 = (bf16[16,16,1024]{2,1,0:T(8,128)(2,1)}, bf16[16,16,1024]{2,1,0:T(8,128)(2,1)S(1)}, u32[]{:S(2)}) copy-start(bf16[16,16,1024]{2,1,0:T(8,128)(2,1)S(1)} %broadcast_select_fusion.1) | copy-start | bytes 1572868
  161.1 6.1 %copy-start.6 = (bf16[256,256]{1,0:T(8,128)(2,1)S(1)}, bf16[256,256]{1,0:T(8,128)(2,1)}, u32[]{:S(2)}) copy-start(bf16[256,256]{1,0:T(8,128)(2,1)} %param.25) | copy-start | bytes 393220
  161.1 6.3 %copy-start.8 = (bf16[256,256]{1,0:T(8,128)(2,1)S(1)}, bf16[256,256]{1,0:T(8,128)(2,1)}, u32[]{:S(2)}) copy-start(bf16[256,256]{1,0:T(8,128)(2,1)} %param.22) | copy-start | bytes 393220
  161.1 7.9 %copy-start.4 = (bf16[16,16,1024]{2,1,0:T(8,128)(2,1)S(1)}, bf16[16,16,1024]{2,1,0:T(8,128)(2,1)}, u32[]{:S(2)}) copy-start(bf16[16,16,1024]{2,1,0:T(8,128)(2,1)} %copy-done.3) | copy-start | bytes 1572868
  161.1 33.3 %all-to-all-start.2 = ((bf16[8,256,512]{2,1,0:T(8,128)(2,1)}), bf16[8,256,512]{2,1,0:T(8,128)(2,1)}, u32[]{:S(2)}, u32[]{:S(2)}) async-start(bf16[8,256,512]{2,1,0:T(8,128)(2,1)} %bitcast.133), calls=%async_computation.2 | async-start | bytes 4194304 | tf_op jit(solution)/shard_map/all_to_all | solution.py:17
  166.6 141.6 %reduce-scatter.3.cloned.1.call-start = ((), (), s32[]{:S(2)}) async-start(), calls=%async_computation.7 | async-start | bytes 8912896 | tf_op jit(solution)/shard_map/reduce_scatter | solution.py:77
  196.7 1.6 copy-start.5
  198.3 36.8 %all-to-all-start.3 = ((bf16[8,256,512]{1,2,0:T(8,128)(2,1)}), bf16[8,256,512]{1,2,0:T(8,128)(2,1)}, u32[]{:S(2)}, u32[]{:S(2)}) async-start(bf16[8,256,512]{1,2,0:T(8,128)(2,1)} %broadcast_in_dim.101), calls=%async_computation.4 | async-start | bytes 4194304 | tf_op jit(solution)/shard_map/all_to_all | solution.py:29
  202.7 175.3 %reduce-scatter.5.cloned.1.call-start = ((), (), s32[]{:S(2)}) async-start(), calls=%async_computation.10 | async-start | bytes 4456448 | tf_op jit(solution)/shard_map/reduce_scatter | solution.py:54
  288.0 3.9 %copy-start.2 = (bf16[8,512,2,128]{3,1,2,0:T(8,128)(2,1)S(1)}, bf16[8,512,2,128]{3,1,2,0:T(8,128)(2,1)}, u32[]{:S(2)}) copy-start(bf16[8,512,2,128]{3,1,2,0:T(8,128)(2,1)} %get-tuple-element.117) | copy-start | bytes 6291460
  300.9 35.9 %all-to-all-start.4 = ((bf16[16,256,256]{1,2,0:T(8,128)(2,1)}), bf16[16,256,256]{1,2,0:T(8,128)(2,1)}, u32[]{:S(2)}, u32[]{:S(2)}) async-start(bf16[16,256,256]{1,2,0:T(8,128)(2,1)} %bitcast.9), calls=%async_computation.5 | async-start | bytes 4194304 | tf_op jit(solution)/shard_map/all_to_all | solution.py:17
  307.4 72.2 %copy-start.1 = (bf16[256,4096]{1,0:T(8,128)(2,1)S(1)}, bf16[256,4096]{1,0:T(8,128)(2,1)}, u32[]{:S(2)}) copy-start(bf16[256,4096]{1,0:T(8,128)(2,1)} %param.19) | copy-start | bytes 6291460
Sparse Core Ops, SparseCore 0:
  11.0 110.3 all-gather.2
  123.8 59.5 all-gather.4
  187.7 104.0 reduce-scatter.2
  297.4 80.5 reduce-scatter.4
